TPU v7x, 32 devices: a whole 2x2x4 slice. The times are simulated.
32 devices in a mesh: rep: 4 (over x, y), dp: 8 (over z, core).
Axes of the slice: x: 2, y: 2, z: 4, core: 2. Of those that a mesh axis runs over, the one named last changes fastest.
Arguments:
- x: bfloat16 [32, 2048, 640], P(('rep', 'dp')), parts along dimension 0
- dy: bfloat16 [32, 2048, 640], P(('rep', 'dp')), parts along dimension 0
- w_gate: bfloat16 [2, 640, 2048], replicated
- w_up: bfloat16 [2, 640, 2048], replicated
- w_down: bfloat16 [2, 2048, 640], replicated
- m_w_gate: float32 [2, 640, 2048], P(None, 'dp')
- m_w_up: float32 [2, 640, 2048], P(None, 'dp')
- m_w_down: float32 [2, 2048, 640], P(None, 'dp')
- v_w_gate: float32 [2, 640, 2048], P(None, 'dp')
- v_w_up: float32 [2, 640, 2048], P(None, 'dp')
- v_w_down: float32 [2, 2048, 640], P(None, 'dp')
Outputs:
- output 1: bfloat16 [8, 640, 2048], P('rep'), parts along dimension 0
- output 2: bfloat16 [8, 640, 2048], P('rep'), parts along dimension 0
- output 3: bfloat16 [8, 2048, 640], P('rep'), parts along dimension 0
- output 4: float32 [8, 640, 2048], P('rep', 'dp'), parts along dimension 0
- output 5: float32 [8, 640, 2048], P('rep', 'dp'), parts along dimension 0
- output 6: float32 [8, 2048, 640], P('rep', 'dp'), parts along dimension 0
- output 7: float32 [8, 640, 2048], P('rep', 'dp'), parts along dimension 0
- output 8: float32 [8, 640, 2048], P('rep', 'dp'), parts along dimension 0
- output 9: float32 [8, 2048, 640], P('rep', 'dp'), parts along dimension 0
There are 4 independent parts. A program takes and returns all parts, laid end to end along the dimension named above; an argument that names none is the same for every part.
All inputs are finite; a program needn't handle non-finite values.
Results may differ from a plain program's by a relative error of at most 0.022.
Values are sent between devices in bfloat16 or wider.
A program may use at most 2 GiB of HBM per device.

v0:
```python
import jax
import jax.numpy as jnp
from jax import lax

NAMES = ("w_gate", "w_up", "w_down")


def matmul(a, w):
    return jnp.dot(a, w, preferred_element_type=jnp.float32).astype(jnp.bfloat16)


def normed(h):
    wide = h.astype(jnp.float32)
    scale = lax.rsqrt(jnp.mean(wide**2, -1, keepdims=True) + 1e-6)
    return (wide * scale).astype(jnp.bfloat16)


def layer(h, w):
    a = normed(h)
    gate = jnp.dot(a, w["w_gate"], preferred_element_type=jnp.float32)
    up = jnp.dot(a, w["w_up"], preferred_element_type=jnp.float32)
    return h + matmul((jax.nn.silu(gate) * up).astype(jnp.bfloat16), w["w_down"])


def adamw(w, m, v, g):
    m = 0.9 * m + 0.1 * g
    v = 0.95 * v + 0.05 * g * g
    step = m * lax.rsqrt(v + 1e-8) + 0.1 * w
    return (w - 0.02 * step).astype(jnp.bfloat16), m, v


def stack(weights, h):
    for number in range(weights["w_gate"].shape[0]):
        h = layer(h, {name: w[number] for name, w in weights.items()})
    return h


def solution(mesh):
    groups = mesh.shape["rep"]

    def step(x, dy, *arrays):
        weights, m, v = (arrays[i : i + 3] for i in (0, 3, 6))
        x, dy = (t.reshape(groups, -1, *t.shape[1:]) for t in (x, dy))

        def of_a_group(x, dy):
            _, back = jax.vjp(lambda w: stack(w, x), dict(zip(NAMES, weights, strict=True)))
            by_weights = back(dy)[0]
            gradients = [by_weights[name].astype(jnp.float32) for name in NAMES]
            new = [adamw(w.astype(jnp.float32), m, v, g) for w, m, v, g in zip(weights, m, v, gradients, strict=True)]
            return tuple(one[which] for which in range(3) for one in new)

        return tuple(t.reshape(-1, *t.shape[2:]) for t in jax.vmap(of_a_group)(x, dy))

    return step
```

profile of v0, /device:TPU:0, one launch (start us, length us, event | category | flops | bytes accessed | tf_op | source)
XLA Modules:
  0.0 657.1 jit_solution(7118804758014149654)
XLA Ops:
  7.2 0.0 reduce-scatter.27.cloned.1.call-start
  7.2 2.5 fusion.35
  9.7 4.4 copy
  14.1 8.6 %fusion.76 = f32[2048,2048]{1,0:T(8,128)S(1)} fusion(bf16[2,640,2048]{2,1,0:T(8,128)(2,1)} %param, bf16[1,2048,640]{2,1,0:T(8,128)(2,1)S(1)} %copy-done.1, f32[2048]{0:T(1024)S(1)} %add_rsqrt_fusion), kind=kOutput, calls=%fused_computation.88 | convolution fusion | flops 5372641280 | bytes 22028288 | tf_op jit(solution)/vmap(jvp())/dot_general | solution.py:20
  22.7 13.6 %fusion.74 = f32[2048,2048]{1,0:T(8,128)} fusion(bf16[2,640,2048]{2,1,0:T(8,128)(2,1)} %param.3, bf16[1,2048,640]{2,1,0:T(8,128)(2,1)S(1)} %copy-done.1, f32[2048]{0:T(1024)S(1)} %add_rsqrt_fusion), kind=kOutput, calls=%fused_computation.86 | convolution fusion | flops 5372641280 | bytes 22028288 | tf_op jit(solution)/vmap(jvp())/dot_general | solution.py:21
  36.3 8.6 %fusion.26 = bf16[2048,2048]{1,0:T(8,128)(2,1)S(1)} fusion(f32[2048,2048]{1,0:T(8,128)} %fusion.74, f32[2048,2048]{1,0:T(8,128)S(1)} %fusion.76), kind=kLoop, calls=%fused_computation.39 | loop fusion | flops 25165824 | bytes 41943040
  44.9 10.1 %fusion.39 = (f32[2048]{0:T(1024)S(1)}, bf16[1,1,2048,640]{2,3,1,0:T(8,128)(2,1)S(1)}) fusion(bf16[2048,2048]{1,0:T(8,128)(2,1)S(1)} %fusion.26, bf16[2,2048,640]{2,1,0:T(8,128)(2,1)} %param.4, bf16[1,2048,640]{1,2,0:T(8,128)(2,1)S(1)} %copy-done.11), kind=kOutput, calls=%fused_computation.56 | convolution fusion | flops 5375260672 | bytes 16261120 | tf_op jit(solution)/vmap(jvp())/dot_general | solution.py:9
  55.0 12.9 %fusion.63 = f32[2048,2048]{1,0:T(8,128)} fusion(bf16[2,640,2048]{2,1,0:T(8,128)(2,1)} %param, bf16[1,1,2048,640]{2,3,1,0:T(8,128)(2,1)S(1)} %get-tuple-element.10, f32[2048]{0:T(1024)S(1)} %bitcast.345), kind=kOutput, calls=%fused_computation.75 | convolution fusion | flops 5372641280 | bytes 22028288 | tf_op jit(solution)/vmap(jvp())/dot_general | solution.py:20
  67.9 12.1 %fusion.66 = f32[2048,2048]{1,0:T(8,128)} fusion(bf16[2,640,2048]{2,1,0:T(8,128)(2,1)} %param.3, bf16[1,1,2048,640]{2,3,1,0:T(8,128)(2,1)S(1)} %get-tuple-element.10, f32[2048]{0:T(1024)S(1)} %bitcast.346), kind=kOutput, calls=%fused_computation.78 | convolution fusion | flops 5372641280 | bytes 22028288 | tf_op jit(solution)/vmap(jvp())/dot_general | solution.py:21
  80.0 16.1 %fusion.42 = f32[1,2048,640]{2,1,0:T(8,128)} fusion(f32[2048,2048]{1,0:T(8,128)} %fusion.66, f32[2048,2048]{1,0:T(8,128)} %fusion.63, bf16[1,2048,640]{2,1,0:T(8,128)(2,1)S(1)} %copy-done.10), kind=kOutput, calls=%fused_computation.61 | convolution fusion | flops 5393874944 | bytes 41418752 | tf_op jit(solution)/vmap(transpose(jvp()))/dot_general | solution.py:9
  96.1 0.0 reduce-scatter.27.cloned.1.call-update
  96.2 0.0 reduce-scatter.29.cloned.1.call-start
  96.2 9.4 %convolution_convert_fusion.1 = bf16[2048,2048]{1,0:T(8,128)(2,1)S(1)} fusion(bf16[1,2048,640]{2,1,0:T(8,128)(2,1)S(1)} %copy-done.10, bf16[2,2048,640]{2,1,0:T(8,128)(2,1)} %param.4), kind=kOutput, calls=%fused_computation.48 | convolution fusion | flops 5372903424 | bytes 13631488 | tf_op jit(solution)/vmap(transpose(jvp()))/dot_general | solution.py:9
  105.7 3.2 copy-done.3
  108.9 15.8 %fusion.6 = bf16[2048,2048]{1,0:T(8,128)(2,1)} fusion(f32[2048,2048]{1,0:T(8,128)} %fusion.63, f32[2048,2048]{1,0:T(8,128)} %fusion.66, bf16[2048,2048]{1,0:T(8,128)(2,1)S(1)} %convolution_convert_fusion.1), kind=kLoop, calls=%fused_computation.11 | loop fusion | flops 50331648 | bytes 50331648
  124.7 3.0 copy.1
  127.7 13.2 %fusion.54 = bf16[2048,640]{0,1:T(8,128)(2,1)} fusion(bf16[2048,2048]{1,0:T(8,128)(2,1)} %copy-done.3, f32[2048,2048]{1,0:T(8,128)} %fusion.63, bf16[2,640,2048]{2,1,0:T(8,128)(2,1)} %param.3), kind=kOutput, calls=%fused_computation.66 | convolution fusion | flops 5395185664 | bytes 30408704 | tf_op jit(solution)/vmap(transpose(jvp()))/dot_general | solution.py:21
  140.9 8.2 %fusion.41 = (f32[2048]{0:T(1024)S(1)}, bf16[2048,640]{0,1:T(8,128)(2,1)S(1)}) fusion(bf16[1,1,2048,640]{2,3,1,0:T(8,128)(2,1)S(1)} %copy-done.7, bf16[2048,640]{0,1:T(8,128)(2,1)} %fusion.54, bf16[2048,2048]{1,0:T(8,128)(2,1)S(1)} %copy-done.4, bf16[2,640,2048]{2,1,0:T(8,128)(2,1)} %param), kind=kOutput, calls=%fused_computation.58 | convolution fusion | flops 5375260672 | bytes 18882560 | tf_op jit(solution)/vmap(transpose(jvp()))/dot_general | solution.py:20
  149.2 1.8 fusion.61
  151.0 1.5 copy-done.9
  152.5 11.0 %convolution_bitcast_fusion.1 = f32[1,2048,640]{2,1,0:T(8,128)} fusion(bf16[2048,2048]{1,0:T(8,128)(2,1)} %copy-done.2, bf16[2048,640]{0,1:T(8,128)(2,1)S(1)} %fusion.61), kind=kOutput, calls=%fused_computation.65 | convolution fusion | flops 5368709120 | bytes 16252928 | tf_op jit(solution)/vmap(transpose(jvp()))/dot_general | solution.py:9
  163.5 0.0 reduce-scatter.29.cloned.1.call-update
  163.5 0.0 reduce-scatter.19.cloned.1.call-start
  163.5 1.7 copy-done.8
  165.2 9.4 %convolution_bitcast_fusion = f32[1,640,2048]{2,1,0:T(8,128)} fusion(bf16[2048,2048]{1,0:T(8,128)(2,1)} %fusion.6, bf16[1,1,2048,640]{2,3,1,0:T(8,128)(2,1)S(1)} %copy-done.8, f32[2048]{0:T(1024)S(1)} %bitcast.348), kind=kOutput, calls=%fused_computation.60 | convolution fusion | flops 5372641280 | bytes 16261120 | tf_op jit(solution)/vmap(transpose(jvp()))/dot_general | solution.py:20
  174.6 0.0 reduce-scatter.19.cloned.1.call-update
  174.7 0.0 reduce-scatter.21.cloned.1.call-start
  174.7 11.2 %convolution_convert_fusion = bf16[2048,2048]{1,0:T(8,128)(2,1)} fusion(bf16[2048,640]{0,1:T(8,128)(2,1)} %copy-done.9, bf16[2,2048,640]{2,1,0:T(8,128)(2,1)} %param.4), kind=kOutput, calls=%fused_computation.47 | convolution fusion | flops 5372903424 | bytes 13631488 | tf_op jit(solution)/vmap(transpose(jvp()))/dot_general | solution.py:9
  185.9 20.7 %fusion.48 = f32[1,640,2048]{2,1,0:T(8,128)} fusion(f32[2048,2048]{1,0:T(8,128)} %copy-done, f32[2048,2048]{1,0:T(8,128)} %fusion.74, bf16[2048,2048]{1,0:T(8,128)(2,1)} %convolution_convert_fusion, bf16[1,2048,640]{1,2,0:T(8,128)(2,1)} %copy, f32[2048]{0:T(1024)S(1)} %copy-done.18), kind=kOutput, calls=%fused_computation.63 | convolution fusion | flops 5418778624 | bytes 49815552 | tf_op jit(solution)/vmap(transpose(jvp()))/dot_general | solution.py:20
  206.6 0.0 reduce-scatter.21.cloned.1.call-update
  206.6 0.0 reduce-scatter.23.cloned.1.call-start
  206.7 12.8 %fusion.45 = f32[1,640,2048]{2,1,0:T(8,128)} fusion(bf16[2048,2048]{1,0:T(8,128)(2,1)} %copy-done.3, f32[2048,2048]{1,0:T(8,128)} %fusion.63, bf16[1,1,2048,640]{2,3,1,0:T(8,128)(2,1)S(1)} %copy-done.8, f32[2048]{0:T(1024)S(1)} %bitcast.349), kind=kOutput, calls=%fused_computation.62 | convolution fusion | flops 5397807104 | bytes 33038336 | tf_op jit(solution)/vmap(transpose(jvp()))/dot_general | solution.py:21
  219.5 0.0 reduce-scatter.23.cloned.1.call-update
  219.5 0.0 reduce-scatter.25.cloned.1.call-start
  219.6 1.7 copy-done.12
  221.3 13.1 %fusion.51 = f32[1,640,2048]{2,1,0:T(8,128)} fusion(bf16[2048,2048]{1,0:T(8,128)(2,1)} %convolution_convert_fusion, f32[2048,2048]{1,0:T(8,128)} %copy-done, bf16[1,2048,640]{1,2,0:T(8,128)(2,1)S(1)} %copy-done.12, f32[2048]{0:T(1024)S(1)} %copy-done.18), kind=kOutput, calls=%fused_computation.64 | convolution fusion | flops 5397807104 | bytes 33038336 | tf_op jit(solution)/vmap(transpose(jvp()))/dot_general | solution.py:21
  234.3 0.0 reduce-scatter.25.cloned.1.call-update
  234.3 0.0 all-gather.14.cloned.1.call-start
  234.4 0.6 copy-done.19
  235.0 0.6 dynamic-slice
  236.2 0.0 reduce-scatter.27.cloned.1.call-done
  236.2 1.1 convert_bitcast_fusion.4
  237.4 0.0 reduce-scatter.29.cloned.1.call-done
  237.4 1.1 convert_bitcast_fusion.3
  238.5 3.5 fusion.124
  242.1 0.0 all-gather.10.cloned.1.call-start
  242.1 45.3 %reduce-scatter.19.cloned.1.call-done = f32[1,80,2048]{2,1,0:T(8,128)} async-done(((f32[1,640,2048]{2,1,0:T(8,128)}), f32[1,80,2048]{2,1,0:T(8,128)}) %reduce-scatter.19.cloned.1.call-update) | async-done | bytes 655376
  287.4 1.1 convert_bitcast_fusion.8
  288.6 60.1 %reduce-scatter.21.cloned.1.call-done = f32[1,80,2048]{2,1,0:T(8,128)} async-done(((f32[1,640,2048]{2,1,0:T(8,128)}), f32[1,80,2048]{2,1,0:T(8,128)}) %reduce-scatter.21.cloned.1.call-update) | async-done | bytes 655376
  348.7 1.1 convert_bitcast_fusion.7
  349.8 4.3 fusion.126
  354.1 0.0 all-gather.10.cloned.1.call-update
  354.1 0.0 all-gather.12.cloned.1.call-start
  354.2 55.2 %reduce-scatter.23.cloned.1.call-done = f32[1,80,2048]{2,1,0:T(8,128)} async-done(((f32[1,640,2048]{2,1,0:T(8,128)}), f32[1,80,2048]{2,1,0:T(8,128)}) %reduce-scatter.23.cloned.1.call-update) | async-done | bytes 655376
  409.4 1.1 convert_bitcast_fusion.6
  410.5 60.1 %reduce-scatter.25.cloned.1.call-done = f32[1,80,2048]{2,1,0:T(8,128)} async-done(((f32[1,640,2048]{2,1,0:T(8,128)}), f32[1,80,2048]{2,1,0:T(8,128)}) %reduce-scatter.25.cloned.1.call-update) | async-done | bytes 655376
  470.7 1.1 convert_bitcast_fusion.5
  471.8 3.5 fusion.125
  475.3 51.1 %all-gather.14.cloned.1.call-done = bf16[1,2,2048,640]{3,2,1,0:T(8,128)(2,1)} async-done(((bf16[1,2,256,640]{3,2,1,0:T(8,128)(2,1)}), bf16[1,2,2048,640]{3,2,1,0:T(8,128)(2,1)}) %all-gather.14.cloned.1.call-update) | async-done | bytes 5242896 | tf_op jit(solution)/reshape | solution.py:52
  526.5 56.4 %all-gather.10.cloned.1.call-done = bf16[1,2,640,2048]{3,2,1,0:T(8,128)(2,1)} async-done(((bf16[1,2,80,2048]{3,2,1,0:T(8,128)(2,1)}), bf16[1,2,640,2048]{3,2,1,0:T(8,128)(2,1)}) %all-gather.10.cloned.1.call-update) | async-done | bytes 5242896 | tf_op jit(solution)/reshape | solution.py:52
  582.9 56.4 %all-gather.12.cloned.1.call-done = bf16[1,2,640,2048]{3,2,1,0:T(8,128)(2,1)} async-done(((bf16[1,2,80,2048]{3,2,1,0:T(8,128)(2,1)}), bf16[1,2,640,2048]{3,2,1,0:T(8,128)(2,1)}) %all-gather.12.cloned.1.call-update) | async-done | bytes 5242896 | tf_op jit(solution)/reshape | solution.py:52
  639.3 6.2 copy.5
  645.5 2.4 copy.6
  647.9 2.4 copy.7
  (46 shorter events, 0.2 us)
Async XLA Ops:
  7.2 6.9 %copy-start.1 = (bf16[1,2048,640]{2,1,0:T(8,128)(2,1)S(1)}, bf16[1,2048,640]{2,1,0:T(8,128)(2,1)}, u32[]{:S(2)}) copy-start(bf16[1,2048,640]{2,1,0:T(8,128)(2,1)} %param.2) | copy-start | bytes 7864324
  7.2 229.0 %reduce-scatter.27.cloned.1.call-start = ((), (), s32[]{:S(2)}) async-start(), calls=%async_computation.13 | async-start | bytes 5898240
  14.1 8.6 %copy-start.17 = (f32[2048]{0:T(1024)}, f32[2048]{0:T(1024)S(1)}, u32[]{:S(2)}) copy-start(f32[2048]{0:T(1024)S(1)} %add_rsqrt_fusion) | copy-start | bytes 24580
  22.7 13.6 %copy-start = (f32[2048,2048]{1,0:T(8,128)}, f32[2048,2048]{1,0:T(8,128)S(1)}, u32[]{:S(2)}) copy-start(f32[2048,2048]{1,0:T(8,128)S(1)} %fusion.76) | copy-start | bytes 50331652
  36.3 8.6 %copy-start.11 = (bf16[1,2048,640]{1,2,0:T(8,128)(2,1)S(1)}, bf16[1,2048,640]{1,2,0:T(8,128)(2,1)}, u32[]{:S(2)}) copy-start(bf16[1,2048,640]{1,2,0:T(8,128)(2,1)} %copy) | copy-start | bytes 7864324
  44.9 10.1 %copy-start.2 = (bf16[2048,2048]{1,0:T(8,128)(2,1)}, bf16[2048,2048]{1,0:T(8,128)(2,1)S(1)}, u32[]{:S(2)}) copy-start(bf16[2048,2048]{1,0:T(8,128)(2,1)S(1)} %fusion.26) | copy-start | bytes 25165828
  55.0 12.9 %copy-start.6 = (bf16[1,1,2048,640]{2,3,1,0:T(8,128)(2,1)}, bf16[1,1,2048,640]{2,3,1,0:T(8,128)(2,1)S(1)}, u32[]{:S(2)}) copy-start(bf16[1,1,2048,640]{2,3,1,0:T(8,128)(2,1)S(1)} %get-tuple-element.10) | copy-start | bytes 7864324
  67.9 12.1 %copy-start.10 = (bf16[1,2048,640]{2,1,0:T(8,128)(2,1)S(1)}, bf16[1,2048,640]{2,1,0:T(8,128)(2,1)}, u32[]{:S(2)}) copy-start(bf16[1,2048,640]{2,1,0:T(8,128)(2,1)} %param.5) | copy-start | bytes 7864324
  96.2 141.2 %reduce-scatter.29.cloned.1.call-start = ((), (), s32[]{:S(2)}) async-start(), calls=%async_computation.14 | async-start | bytes 5898240
  105.7 3.2 copy-start.3
  127.7 13.2 %copy-start.4 = (bf16[2048,2048]{1,0:T(8,128)(2,1)S(1)}, bf16[2048,2048]{1,0:T(8,128)(2,1)}, u32[]{:S(2)}) copy-start(bf16[2048,2048]{1,0:T(8,128)(2,1)} %fusion.6) | copy-start | bytes 25165828
  127.7 13.2 %copy-start.7 = (bf16[1,1,2048,640]{2,3,1,0:T(8,128)(2,1)S(1)}, bf16[1,1,2048,640]{2,3,1,0:T(8,128)(2,1)}, u32[]{:S(2)}) copy-start(bf16[1,1,2048,640]{2,3,1,0:T(8,128)(2,1)} %copy-done.6) | copy-start | bytes 7864324
  151.0 1.5 copy-start.9
  163.5 1.7 copy-start.8
  163.5 124.0 %reduce-scatter.19.cloned.1.call-start = ((), (), s32[]{:S(2)}) async-start(), calls=%async_computation.9 | async-start | bytes 5898240
  174.7 11.3 %copy-start.18 = (f32[2048]{0:T(1024)S(1)}, f32[2048]{0:T(1024)}, u32[]{:S(2)}) copy-start(f32[2048]{0:T(1024)} %copy-done.17) | copy-start | bytes 24580
  174.7 174.0 %reduce-scatter.21.cloned.1.call-start = ((), (), s32[]{:S(2)}) async-start(), calls=%async_computation.10 | async-start | bytes 5898240
  206.6 202.8 %reduce-scatter.23.cloned.1.call-start = ((), (), s32[]{:S(2)}) async-start(), calls=%async_computation.11 | async-start | bytes 5898240
  219.5 1.7 copy-start.12
  219.5 251.1 %reduce-scatter.25.cloned.1.call-start = ((), (), s32[]{:S(2)}) async-start(), calls=%async_computation.12 | async-start | bytes 5898240
  234.3 0.7 copy-start.19
  234.3 4.2 copy-start.13
  234.3 4.2 copy-start.14
  234.3 292.1 %all-gather.14.cloned.1.call-start = ((), (), s32[]{:S(2)}) async-start(), calls=%async_computation.8 | async-start | bytes 5898240 | tf_op jit(solution)/reshape | solution.py:52
  242.1 340.8 %all-gather.10.cloned.1.call-start = ((), (), s32[]{:S(2)}) async-start(), calls=%async_computation.6 | async-start | bytes 5898240 | tf_op jit(solution)/reshape | solution.py:52
  288.6 183.2 %copy-start.15 = (f32[2,80,2048]{2,1,0:T(8,128)S(1)}, f32[2,80,2048]{2,1,0:T(8,128)}, u32[]{:S(2)}) copy-start(f32[2,80,2048]{2,1,0:T(8,128)} %param.8) | copy-start | bytes 3932164
  288.6 183.2 %copy-start.16 = (f32[2,80,2048]{2,1,0:T(8,128)S(1)}, f32[2,80,2048]{2,1,0:T(8,128)}, u32[]{:S(2)}) copy-start(f32[2,80,2048]{2,1,0:T(8,128)} %param.7) | copy-start | bytes 3932164
  354.1 285.2 %all-gather.12.cloned.1.call-start = ((), (), s32[]{:S(2)}) async-start(), calls=%async_computation.7 | async-start | bytes 5898240 | tf_op jit(solution)/reshape | solution.py:52
  639.3 6.2 copy-start.5
  639.3 8.5 %slice-start = ((s8[5242880]{0:T(1024)(128)(4,1)}), s8[4194304]{0:T(1024)(128)(4,1)S(1)}, s32[]{:S(2)}) async-start(s8[5242880]{0:T(1024)(128)(4,1)} %bitcast.337), calls=%async_computation.15 | async-start | bytes 8388608
  645.5 2.4 slice-start.1
Sparse Core Ops, SparseCore 0:
  96.3 62.3 reduce-scatter.26
  163.6 62.3 reduce-scatter.28
  228.9 58.4 reduce-scatter.18
  290.2 58.4 reduce-scatter.20
  350.8 58.5 reduce-scatter.22
  412.1 58.4 reduce-scatter.24
  472.3 54.1 all-gather.13
  528.6 54.2 all-gather.9
  585.1 54.2 all-gather.11
where the time goes:
time: 667 us; the launch traced here: 657 us
  waiting for transfers between devices  385 us (58%)
  matrix products  182 us (27%)
  other arithmetic  46.8 us (7%)
  local copies, waits for them, and re-layouts  27.5 us (4%)
  between operations  15.2 us (2%)
    unnamed x15, waiting for transfers between devices  221 us
    reshape x3, waiting for transfers between devices, step(): t.reshape(-1, *t.shape[2:])  164 us
    dot_general x5, matrix products, layer(): up = jnp.dot(a, w['w_up'], preferred_element_type=jnp.float32)  64.8 us
    dot_general x5, matrix products, layer(): gate = jnp.dot(a, w['w_gate'], preferred_element_type=jnp.float32)  59.8 us
    dot_general x5, matrix products, matmul(): jnp.dot(a, w, preferred_element_type=jnp.float32).astype(jnp.bfloat16)  57.8 us
    unnamed x49, local copies, waits for them, and re-layouts  26.9 us
    unnamed x4, other arithmetic  26.2 us
  transfers between devices with their start and end apart: 9, of which 7 were waited for; matrix products, arithmetic and copies ran while one was open for 23% of the time, Pallas kernels for 0%

commit v1 on v0

v1 whole, which is shorter than its diff:
```python
import functools

import jax
import jax.numpy as jnp
from jax import lax
from jax.experimental import pallas as pl
from jax.experimental.pallas import tpu as pltpu
from jax.sharding import PartitionSpec as P

D, FF, CHUNKS = 640, 2048, 16
BF, F32 = jnp.bfloat16, jnp.float32
SLOTS = 4


def normed(h):
    wide = h.astype(F32)
    scale = lax.rsqrt(jnp.mean(wide**2, -1, keepdims=True) + 1e-6)
    return (wide * scale).astype(BF)


def dot(a, b):
    return lax.dot_general(a, b, (((1,), (0,)), ((), ())), preferred_element_type=F32)


def dot_t(a, b):
    return lax.dot_general(a, b, (((1,), (1,)), ((), ())), preferred_element_type=F32)


def where(j):
    layer, s, h = 1 - j // 8, j % 4, (j // 4) % 2
    first = pl.multiple_of(s * 512 + h * 128, 128)
    return layer, s, h, first, pl.multiple_of(first + 256, 128)


def adam(w, m, v, g):
    m = 0.9 * m + 0.1 * g
    v = 0.95 * v + 0.05 * g * g
    return (w - 0.02 * (m * lax.rsqrt(v + 1e-8) + 0.1 * w)).astype(BF), m, v


def kernel(tile, a1, a0, h1, dy, wg, wu, wd, og, ou, od, mg, mu, md, vg, vu, vd,
           ng, nu, nd, pmg, pmu, pmd, pvg, pvu, pvd,
           a_s, at_s, do_s, dot_s, h_s, da_s, act_s, dg_s, du_s, wgb, wub, wdb, gg, gu, gd,
           pg, pd, d2s_g, d2s_d, d2r_g, d2r_d, sr_g, sr_d, sl_g, sl_d, rl_g, rl_d, rr_g, rr_d, nw_g, nw_d,
           wsem, lsem, d2_ss, d2_rs, sr_ss, rl_rs, sl_ss, rr_rs, own_s, ar_ss, al_ss, ap_ss, al_rs, ar_rs, ap_rs):
    dev = lax.axis_index("dp")
    z, k = dev // 2, dev % 2
    right, left, other = {"dp": (dev + 2) % 8}, {"dp": (dev + 6) % 8}, {"dp": z * 2 + 1 - k}
    tiles = a_s.shape[0] // tile

    barrier = pltpu.get_barrier_semaphore()
    for to in (right, left, other):
        pl.semaphore_signal(barrier, inc=1, device_id=to, device_id_type=pl.DeviceIdType.MESH)
    pl.semaphore_wait(barrier, 3)

    def remote(src, dst, ss, rs, to):
        return pltpu.make_async_remote_copy(src_ref=src, dst_ref=dst, send_sem=ss, recv_sem=rs, device_id=to,
                                            device_id_type=pl.DeviceIdType.MESH)

    def ok(j):
        return (j >= 0) & (j < CHUNKS)

    def weights(j):
        layer, _, _, c1, c2 = where(j)
        slot = j % 2
        out = []
        for i, c in enumerate((c1, c2)):
            here = slice(128 * i, 128 * i + 128)
            out.append((wg.at[layer, :, pl.ds(c, 128)], wgb.at[slot, :, here]))
            out.append((wu.at[layer, :, pl.ds(c, 128)], wub.at[slot, :, here]))
            out.append((wd.at[layer, pl.ds(c, 128), :], wdb.at[slot, here, :]))
        return [pltpu.make_async_copy(src, dst, wsem.at[slot, i]) for i, (src, dst) in enumerate(out)]

    def over_tiles(body):
        @pl.loop(0, tiles)
        def _(i):
            body(pl.ds(pl.multiple_of(i * tile, tile), tile))

    first = [pltpu.make_async_copy(a1, a_s, lsem.at[0]), pltpu.make_async_copy(dy, do_s, lsem.at[1]),
             pltpu.make_async_copy(h1, h_s, lsem.at[2])]
    for c in first + weights(0):
        c.start()
    for c in first:
        c.wait()

    def chunk(t):
        slot = t % 2

        @pl.when(t == 8)
        def _():
            fetch = pltpu.make_async_copy(a0, a_s, lsem.at[0])
            fetch.start()

            def back(rows):
                h = h_s[rows, :].astype(F32)
                da = da_s[rows, :].astype(BF).astype(F32)
                r = lax.rsqrt(jnp.mean(h * h, -1, keepdims=True) + 1e-6)
                dh = r * da - h * (r * r * r * jnp.mean(h * da, -1, keepdims=True))
                do_s[rows, :] = (do_s[rows, :].astype(F32) + dh.astype(BF).astype(F32)).astype(BF)

            over_tiles(back)
            fetch.wait()

        @pl.when((t == 0) | (t == 8))
        def _():
            def turn(rows):
                at_s[:, rows] = a_s[rows, :].T
                dot_s[:, rows] = do_s[rows, :].T
                da_s[rows, :] = jnp.zeros((tile, D), F32)

            over_tiles(turn)

        for c in weights(t):
            c.wait()

        @pl.when(t + 1 < CHUNKS)
        def _():
            for c in weights(t + 1):
                c.start()

        def through(rows):
            a, d = a_s[rows, :], do_s[rows, :]
            gate, up = dot(a, wgb[slot]), dot(a, wub[slot])
            dact = dot_t(d, wdb[slot]).astype(BF).astype(F32)
            sig = jax.nn.sigmoid(gate)
            silu = gate * sig
            act_s[rows, :] = (silu * up).astype(BF)
            du_s[rows, :] = (dact * silu).astype(BF)
            dg_s[rows, :] = (dact * up * (sig * (1 + gate * (1 - sig)))).astype(BF)

        over_tiles(through)

        @pl.when(t < 8)
        def _():
            def into(rows):
                da_s[rows, :] += dot_t(dg_s[rows, :], wgb[slot]) + dot_t(du_s[rows, :], wub[slot])

            over_tiles(into)

    def gradients(t):
        slot, keep = t % 2, t % SLOTS
        gg[...] = dot(at_s[...], dg_s[...])
        gu[...] = dot(at_s[...], du_s[...])
        gd[...] = dot(dot_s[...], act_s[...])
        for b in range(4):
            mine = pl.ds(pl.multiple_of(160 * b + 80 * k, 16), 80)
            its = pl.ds(pl.multiple_of(160 * b + 80 * (1 - k), 16), 80)
            for i, g in enumerate((gg, gu)):
                pg[keep, b, 80 * i : 80 * i + 80, :] = g[mine, :]
                d2s_g[slot, b, 80 * i : 80 * i + 80, :] = g[its, :].astype(BF)
        pd[keep] = gd[:, pl.ds(pl.multiple_of(128 * k, 128), 128)].T
        d2s_d[slot] = gd[:, pl.ds(pl.multiple_of(128 * (1 - k), 128), 128)].T.astype(BF)
        for c in swap(t):
            c.start()

    def swap(j):
        slot, keep = j % 2, j % SLOTS
        return [remote(d2s_g.at[slot], d2r_g.at[keep], d2_ss.at[slot, 0], d2_rs.at[keep, 0], other),
                remote(d2s_d.at[slot], d2r_d.at[keep], d2_ss.at[slot, 1], d2_rs.at[keep, 1], other)]

    def to_right(j, b):
        return remote(sr_g.at[j % 2, b - 1], rl_g.at[j % SLOTS, b - 1], sr_ss.at[j % 2, b - 1], rl_rs.at[j % SLOTS, b - 1], right)

    def to_right_d(j):
        return remote(sr_d.at[j % 2], rl_d.at[j % SLOTS], sr_ss.at[j % 2, 3], rl_rs.at[j % SLOTS, 3], right)

    def to_left(j, b):
        return remote(sl_g.at[j % 2, b], rr_g.at[j % SLOTS, b], sl_ss.at[j % 2, b], rr_rs.at[j % SLOTS, b], left)

    def to_left_d(j):
        return remote(sl_d.at[j % 2], rr_d.at[j % SLOTS], sl_ss.at[j % 2, 3], rr_rs.at[j % SLOTS, 3], left)

    def reduce(t):
        j = t - 1

        @pl.when(ok(j))
        def _():
            for c in swap(j):
                c.wait()
            keep = j % SLOTS
            for b in range(4):
                pg[keep, b] += d2r_g[keep, b].astype(F32)
            pd[keep] += d2r_d[keep].astype(F32)

        def rightward(j, act):
            s = where(j)[1]
            for b in (1, 2, 3):
                pl.when(ok(j) & (z < b) & (z < 3))(lambda b=b: act(b))
            pl.when(ok(j) & (z < 3) & (z < s))(lambda: act(None))

        def leftward(j, act):
            s = where(j)[1]
            for b in (0, 1, 2):
                pl.when(ok(j) & (z > b) & (z > 0))(lambda b=b: act(b))
            pl.when(ok(j) & (z > 0) & (z > s))(lambda: act(None))

        jr = t - 1 - z
        s = where(jr)[1]
        for b in (1, 2, 3):
            @pl.when(ok(jr) & (z > 0) & (z <= b))
            def _():
                to_right(jr, b).wait_recv()
                pg[jr % SLOTS, b] += rl_g[jr % SLOTS, b - 1].astype(F32)

        @pl.when(ok(jr) & (z > 0) & (z <= s))
        def _():
            to_right_d(jr).wait_recv()
            pd[jr % SLOTS] += rl_d[jr % SLOTS].astype(F32)

        def send_r(b):
            if b is None:
                sr_d[jr % 2] = pd[jr % SLOTS].astype(BF)
                to_right_d(jr).start()
            else:
                sr_g[jr % 2, b - 1] = pg[jr % SLOTS, b].astype(BF)
                to_right(jr, b).start()

        rightward(jr, send_r)
        rightward(jr - 1, lambda b: (to_right_d(jr - 1) if b is None else to_right(jr - 1, b)).wait_send())

        jl = t - 4 + z
        s = where(jl)[1]
        for b in (0, 1, 2):
            @pl.when(ok(jl) & (z < 3) & (z >= b))
            def _():
                to_left(jl, b).wait_recv()
                pg[jl % SLOTS, b] += rr_g[jl % SLOTS, b].astype(F32)

        @pl.when(ok(jl) & (z < 3) & (z >= s))
        def _():
            to_left_d(jl).wait_recv()
            pd[jl % SLOTS] += rr_d[jl % SLOTS].astype(F32)

        def send_l(b):
            if b is None:
                sl_d[jl % 2] = pd[jl % SLOTS].astype(BF)
                to_left_d(jl).start()
            else:
                sl_g[jl % 2, b] = pg[jl % SLOTS, b].astype(BF)
                to_left(jl, b).start()

        leftward(jl, send_l)
        leftward(jl - 1, lambda b: (to_left_d(jl - 1) if b is None else to_left(jl - 1, b)).wait_send())

    def update(j):
        layer, s, h, c1, c2 = where(j)
        keep, slot = j % SLOTS, j % 2
        for i, (w, m, v, pm, pv) in enumerate(((og, mg, vg, pmg, pvg), (ou, mu, vu, pmu, pvu))):
            for n, c in enumerate((c1, c2)):
                at = (layer, slice(None), pl.ds(c, 128))
                g = pg[keep, z, 80 * i : 80 * i + 80, 128 * n : 128 * n + 128].astype(BF).astype(F32)
                new, pm[at], pv[at] = adam(w[at].astype(F32), m[at], v[at], g)
                nw_g[slot, 80 * i : 80 * i + 80, 128 * n : 128 * n + 128] = new

        @pl.when(s == z)
        def _():
            at = (layer, pl.ds(pl.multiple_of(h * 128, 128), 128), slice(None))
            g = pd[keep].astype(BF).astype(F32)
            new, pmd[at], pvd[at] = adam(od[at].astype(F32), md[at], vd[at], g)
            nw_d[slot] = new

    def windows(j, origin, core):
        layer, s, h, c1, c2 = where(j)
        rows = pl.ds(pl.multiple_of(160 * origin + 80 * core, 16), 80)
        down = pl.ds(pl.multiple_of((2 * origin + core) * 256 + 128 * h, 128), 128)
        return [n.at[layer, rows, pl.ds(c, 128)] for n in (ng, nu) for c in (c1, c2)], nd.at[layer, down, :], s == origin

    def sources(j, a, origin):
        if a == 0:
            slot = j % 2
            return [nw_g.at[slot, 80 * i : 80 * i + 80, 128 * n : 128 * n + 128] for i in range(2) for n in range(2)], nw_d.at[slot]
        return windows(j, origin, k)[:2]

    def start(j, a, origin, ss, rs, to):
        into, into_d, has = windows(j, origin, k)
        src, src_d = sources(j, a, origin)
        for x, y in zip(src, into, strict=True):
            remote(x, y, ss.at[j % 2, a, 0], rs.at[j % SLOTS, a, 0], to).start()

        @pl.when(has)
        def _():
            remote(src_d, into_d, ss.at[j % 2, a, 1], rs.at[j % SLOTS, a, 1], to).start()

    def finish(has, gate_up, down):
        pltpu.make_async_copy(nw_g.at[0], nw_g.at[0], gate_up).wait()

        @pl.when(has)
        def _():
            pltpu.make_async_copy(nw_d.at[0], nw_d.at[0], down).wait()

    def gather(t):
        def each(j, a, origin, side, what):
            valid = ok(j) & (origin >= 0) & (origin < 4)
            has = where(j)[1] == origin

            @pl.when(valid)
            def _():
                if side in (0, 1) and a < 3:
                    pl.when(z < 3)(lambda: what(j, a, origin, has, ar_ss, al_rs, right))
                if side in (0, 2) and a < 3:
                    pl.when(z > 0)(lambda: what(j, a, origin, has, al_ss, ar_rs, left))
                what(j, a, origin, has, ap_ss.at[side], ap_rs.at[side], other)

        def waited(j, a, origin, has, ss, rs, to):
            finish(has, ss.at[j % 2, a, 0], ss.at[j % 2, a, 1])

        def begun(j, a, origin, has, ss, rs, to):
            start(j, a, origin, ss, rs, to)

        j = t - 4

        @pl.when(ok(j - 1))
        def _():
            finish(where(j - 1)[1] == z, own_s.at[(j - 1) % 2, 0], own_s.at[(j - 1) % 2, 1])

        each(j - 1, 0, z, 0, waited)

        @pl.when(ok(j))
        def _():
            update(j)
            into, into_d, has = windows(j, z, k)
            src, src_d = sources(j, 0, z)
            for x, y in zip(src, into, strict=True):
                pltpu.make_async_copy(x, y, own_s.at[j % 2, 0]).start()

            @pl.when(has)
            def _():
                pltpu.make_async_copy(src_d, into_d, own_s.at[j % 2, 1]).start()

        each(j, 0, z, 0, begun)

        for a in (1, 2, 3):
            ja = t - 4 - a
            for side, origin, rs in ((1, z - a, al_rs), (2, z + a, ar_rs)):
                each(ja - 1, a, origin, side, waited)

                @pl.when(ok(ja) & (origin >= 0) & (origin < 4))
                def _():
                    finish(where(ja)[1] == origin, rs.at[ja % SLOTS, a - 1, 0], rs.at[ja % SLOTS, a - 1, 1])

                each(ja, a, origin, side, begun)

        for a in (0, 1, 2, 3):
            jp = t - 5 - a
            for side, origin in ((0, z),) if a == 0 else ((1, z - a), (2, z + a)):
                @pl.when(ok(jp) & (origin >= 0) & (origin < 4))
                def _():
                    finish(where(jp)[1] == origin, ap_rs.at[side, jp % SLOTS, a, 0], ap_rs.at[side, jp % SLOTS, a, 1])

    @pl.loop(0, CHUNKS + 8)
    def _(t):
        pl.when(t < CHUNKS)(lambda: chunk(t))
        reduce(t)
        gather(t)
        pl.when(t < CHUNKS)(lambda: gradients(t))


def step_kernel(tokens):
    tile = min(tokens, 512)
    sds = jax.ShapeDtypeStruct
    hbm, vmem = pl.BlockSpec(memory_space=pltpu.HBM), pl.BlockSpec(memory_space=pltpu.VMEM)
    wide, tall, block, down = (2, D, FF), (2, FF, D), (2, D // 8, FF), (2, FF // 8, D)
    gu, dn = (160, 256), (128, D)
    V, dma = pltpu.VMEM, pltpu.SemaphoreType.DMA
    scratch = [
        V((tokens, D), BF), V((D, tokens), BF), V((tokens, D), BF), V((D, tokens), BF), V((tokens, D), BF), V((tokens, D), F32),
        V((tokens, 256), BF), V((tokens, 256), BF), V((tokens, 256), BF),
        V((2, D, 256), BF), V((2, D, 256), BF), V((2, 256, D), BF), V((D, 256), F32), V((D, 256), F32), V((D, 256), F32),
        V((SLOTS, 4, *gu), F32), V((SLOTS, *dn), F32), V((2, 4, *gu), BF), V((2, *dn), BF), V((SLOTS, 4, *gu), BF), V((SLOTS, *dn), BF),
        V((2, 3, *gu), BF), V((2, *dn), BF), V((2, 3, *gu), BF), V((2, *dn), BF),
        V((SLOTS, 3, *gu), BF), V((SLOTS, *dn), BF), V((SLOTS, 3, *gu), BF), V((SLOTS, *dn), BF),
        V((2, *gu), BF), V((2, *dn), BF),
        dma((2, 6)), dma((3,)), dma((2, 2)), dma((SLOTS, 2)), dma((2, 4)), dma((SLOTS, 4)), dma((2, 4)), dma((SLOTS, 4)),
        dma((2, 2)), dma((2, 3, 2)), dma((2, 3, 2)), dma((3, 2, 4, 2)), dma((SLOTS, 3, 2)), dma((SLOTS, 3, 2)), dma((3, SLOTS, 4, 2)),
    ]
    return pl.pallas_call(
        functools.partial(kernel, tile),
        out_shape=[sds(wide, BF), sds(wide, BF), sds(tall, BF)] + [sds(s, F32) for s in (block, block, down)] * 2,
        in_specs=[hbm] * 7 + [vmem] * 9,
        out_specs=[hbm] * 3 + [vmem] * 6,
        scratch_shapes=scratch,
        compiler_params=pltpu.CompilerParams(collective_id=0, has_side_effects=True, vmem_limit_bytes=64 * 2**20),
        name="step",
    )


def solution(mesh):
    def step(x, dy, wg, wu, wd, *moments):
        x, dy = x[0], dy[0]
        a0 = normed(x)
        gate = dot(a0, wg[0])
        up = dot(a0, wu[0])
        h1 = x + dot((jax.nn.silu(gate) * up).astype(BF), wd[0]).astype(BF)
        a1 = normed(h1)
        me = lax.axis_index("dp")
        own = [lax.dynamic_slice_in_dim(w, me * (w.shape[1] // 8), w.shape[1] // 8, 1) for w in (wg, wu, wd)]
        return tuple(step_kernel(x.shape[0])(a1, a0, h1, dy, wg, wu, wd, *own, *moments))

    mine, whole, rows = P(("rep", "dp"), None, None), P(None, None, None), P(None, "dp", None)
    return jax.shard_map(
        step, mesh=mesh, in_specs=(mine, mine) + (whole,) * 3 + (rows,) * 6,
        out_specs=(P("rep", None, None),) * 3 + (P("rep", "dp", None),) * 6, check_vma=False,
    )
```

time: 667 us -> 321 us (0.48); the launches traced: 657 us -> 321 us
  waiting for transfers between devices: 385 us -> 0 us
  Pallas kernels: 0 us -> 257 us
  matrix products: 182 us -> 33.5 us
  other arithmetic: 46.8 us -> 7.61 us
  between operations: 15.2 us -> 0.73 us
    pallas_call x0 -> x1, Pallas kernels: none -> 257 us  [step(): step_kernel(x.shape[0])(a1, a0, h1, dy, wg, wu, wd, *own, *moments)]
    unnamed x15 -> x0, waiting for transfers between devices: 221 us -> none
    reshape x3 -> x0, waiting for transfers between devices: 164 us -> none  [step(): t.reshape(-1, *t.shape[2:])]
    dot_general x15 -> x2, matrix products: 182 us -> 33.5 us  [dot(): lax.dot_general(a, b, (((1,), (0,)), ((), ())), preferred_element_type=F32)]
    unnamed x4 -> x1, other arithmetic: 26.2 us -> 0.01 us
    reshape x3 -> x0, other arithmetic: 11.3 us -> none  [step(): t.reshape(-1, *t.shape[2:])]
    unnamed x49 -> x31, local copies, waits for them, and re-layouts: 26.9 us -> 17.6 us
    broadcast_in_dim x6 -> x0, other arithmetic: 6.74 us -> none  [stack(): h = layer(h, {name: w[number] for name, w in weights.items()})]
  transfers between devices with their start and end apart: 9 -> 0, of which waited for: 7 -> 0; matrix products, arithmetic and copies ran while one was open for 23% -> 0% of each run, Pallas kernels for 0% -> 0%
where the time goes in v1:
time: 321 us
  Pallas kernels  257 us (80%)
  matrix products  33.5 us (10%)
  local copies, waits for them, and re-layouts  22 us (7%)
  other arithmetic  7.61 us (2%)
    pallas_call x1, Pallas kernels, step(): step_kernel(x.shape[0])(a1, a0, h1, dy, wg, wu, wd, *own, *moments)  257 us
    dot_general x2, matrix products, dot(): lax.dot_general(a, b, (((1,), (0,)), ((), ())), preferred_element_type=F32)  33.5 us
    unnamed x31, local copies, waits for them, and re-layouts  17.6 us

profile of v1, /device:TPU:0, one launch (start us, length us, event | category | flops | bytes accessed | tf_op | source)
XLA Modules:
  0.0 320.9 jit_solution(15385954594985711651)
XLA Ops:
  0.6 0.0 copy-start.1
  0.7 2.5 fusion
  3.1 2.0 constant_dynamic-slice_fusion.od
  5.1 2.5 constant_dynamic-slice_fusion.1
  7.6 0.0 copy-done.1
  7.6 11.6 %fusion.9 = f32[2048,2048]{1,0:T(8,128)} fusion(bf16[2,640,2048]{2,1,0:T(8,128)(2,1)} %wg.1, bf16[1,2048,640]{2,1,0:T(8,128)(2,1)S(1)} %copy-done.1, f32[2048]{0:T(1024)S(1)} %add_rsqrt_fusion.1), kind=kOutput, calls=%fused_computation.14 | convolution fusion | flops 5372641280 | bytes 22028288 | tf_op jit(solution)/shard_map/dot_general | solution.py:22
  19.2 21.9 %fusion.2 = (f32[2048]{0:T(1024)S(1)}, bf16[2048,640]{1,0:T(8,128)(2,1)S(1)}) fusion(bf16[2,2048,640]{2,1,0:T(8,128)(2,1)} %wd.1, f32[2048,2048]{1,0:T(8,128)} %fusion.9, bf16[2,640,2048]{2,1,0:T(8,128)(2,1)} %wu.1, bf16[1,2048,640]{2,1,0:T(8,128)(2,1)} %param.11, f32[2048]{0:T(1024)S(1)} %add_rsqrt_fusion.1), kind=kOutput, calls=%fused_computation.7 | convolution fusion | flops 10776999936 | bytes 29900800 | tf_op jit(solution)/shard_map/dot_general | solution.py:22
  41.1 0.0 copy-start
  41.1 5.1 %fusion.1 = (bf16[2048,640]{1,0:T(8,128)(2,1)}, bf16[2048,640]{1,0:T(8,128)(2,1)}) fusion(bf16[1,2048,640]{2,1,0:T(8,128)(2,1)} %param.11, f32[2048]{0:T(1024)S(1)} %add_rsqrt_fusion.1, f32[2048]{0:T(1024)S(1)} %add_rsqrt_fusion, bf16[2048,640]{1,0:T(8,128)(2,1)S(1)} %get-tuple-element.10.h1), kind=kLoop, calls=%fused_computation.6 | loop fusion | flops 7864320 | bytes 10502144 | tf_op jit(solution)/shard_map/convert_element_type | solution.py:18
  46.2 0.0 copy-done
  46.2 257.1 %step.1 = (bf16[2,640,2048]{2,1,0:T(8,128)(2,1)}, bf16[2,640,2048]{2,1,0:T(8,128)(2,1)}, bf16[2,2048,640]{2,1,0:T(8,128)(2,1)}, f32[2,80,2048]{2,1,0:T(8,128)}, ...) custom-call(bf16[2048,640]{1,0:T(8,128)(2,1)} %get-tuple-element.14., ...), custom_call_target="tpu_custom_call" | custom-call | tf_op jit(solution)/shard_map/step/pallas_call | solution.py:397
  303.3 0.0 copy-start.2
  303.4 0.0 slice-start
  303.4 6.2 %copy.31 = bf16[2,640,2048]{2,1,0:T(8,128)(2,1)} copy(bf16[2,640,2048]{2,1,0:T(8,128)(2,1)} %get-tuple-element.24) | data formatting | bytes 10485760
  309.5 0.0 copy-done.2
  309.5 0.0 slice-start.1
  309.5 2.4 copy.32
  311.9 0.0 slice-done
  311.9 0.0 slice-done.1
  311.9 0.0 copy-start.8
  311.9 0.0 copy-start.7
  311.9 2.7 copy.33
  314.6 0.0 copy-done.8
  314.6 0.0 copy-start.6
  314.6 0.0 copy-start.5
  314.6 0.0 copy-start.4
  314.6 1.1 copy.34
  315.6 0.0 copy-done.7
  315.6 0.0 copy-start.3
  315.6 1.1 copy.35
  316.7 0.0 copy-done.6
  316.7 1.1 copy.36
  317.8 0.0 copy-done.5
  317.8 1.1 copy.37
  318.8 0.0 copy-done.4
  318.8 1.1 copy.38
  319.9 0.0 copy-done.3
  319.9 1.1 copy.39
  (3 shorter events, 0.0 us)
Async XLA Ops:
  0.6 7.0 %copy-start.1 = (bf16[1,2048,640]{2,1,0:T(8,128)(2,1)S(1)}, bf16[1,2048,640]{2,1,0:T(8,128)(2,1)}, u32[]{:S(2)}) copy-start(bf16[1,2048,640]{2,1,0:T(8,128)(2,1)} %param.11) | copy-start | bytes 7864324
  41.1 5.1 %copy-start = (bf16[2048,640]{1,0:T(8,128)(2,1)}, bf16[2048,640]{1,0:T(8,128)(2,1)S(1)}, u32[]{:S(2)}) copy-start(bf16[2048,640]{1,0:T(8,128)(2,1)S(1)} %get-tuple-element.10.h1) | copy-start | bytes 7864324
  303.3 6.2 %copy-start.2 = (bf16[2,640,2048]{2,1,0:T(8,128)(2,1)S(1)}, bf16[2,640,2048]{2,1,0:T(8,128)(2,1)}, u32[]{:S(2)}) copy-start(bf16[2,640,2048]{2,1,0:T(8,128)(2,1)} %get-tuple-element.25) | copy-start | bytes 15728644
  303.4 8.5 %slice-start = ((s8[5242880]{0:T(1024)(128)(4,1)}), s8[4194304]{0:T(1024)(128)(4,1)S(1)}, s32[]{:S(2)}) async-start(s8[5242880]{0:T(1024)(128)(4,1)} %bitcast.31), calls=%async_computation | async-start | bytes 8388608
  309.5 2.4 slice-start.1
  311.9 2.7 copy-start.8
  311.9 3.8 %copy-start.7 = (f32[2,80,2048]{2,1,0:T(8,128)S(1)}, f32[2,80,2048]{2,1,0:T(8,128)}, u32[]{:S(2)}) copy-start(f32[2,80,2048]{2,1,0:T(8,128)} %get-tuple-element.28) | copy-start | bytes 3932164
  314.6 2.1 copy-start.6
  314.6 3.2 copy-start.5
  314.6 4.2 %copy-start.4 = (f32[2,80,2048]{2,1,0:T(8,128)S(1)}, f32[2,80,2048]{2,1,0:T(8,128)}, u32[]{:S(2)}) copy-start(f32[2,80,2048]{2,1,0:T(8,128)} %get-tuple-element.31) | copy-start | bytes 3932164
  315.6 4.2 %copy-start.3 = (f32[2,256,640]{2,1,0:T(8,128)S(1)}, f32[2,256,640]{2,1,0:T(8,128)}, u32[]{:S(2)}) copy-start(f32[2,256,640]{2,1,0:T(8,128)} %get-tuple-element.32) | copy-start | bytes 3932164

commit v2 on v1

v2 whole, which is shorter than its diff:
```python
import functools

import jax
import jax.numpy as jnp
from jax import lax
from jax.experimental import pallas as pl
from jax.experimental.pallas import tpu as pltpu
from jax.sharding import PartitionSpec as P

D, FF, CHUNKS = 640, 2048, 16
BF, F32 = jnp.bfloat16, jnp.float32
SLOTS = 4
HELD = 5


def dot(a, b):
    return lax.dot_general(a, b, (((1,), (0,)), ((), ())), preferred_element_type=F32)


def dot_t(a, b):
    return lax.dot_general(a, b, (((1,), (1,)), ((), ())), preferred_element_type=F32)


def where(j):
    layer, h = 1 - j // 8, j % 2
    c1 = chip_of(j, 0) * 512 + h * 128
    c2 = chip_of(j, 1) * 512 + 256 + h * 128
    return layer, h, pl.multiple_of(c1, 128), pl.multiple_of(c2, 128)


def chip_of(j, core):
    s = (j // 2 + 3 - 2 * (j // 8)) % 4
    return s + core * (3 - 2 * s)


def adam(w, m, v, g):
    m = 0.9 * m + 0.1 * g
    v = 0.95 * v + 0.05 * g * g
    return (w - 0.02 * (m * lax.rsqrt(v + 1e-8) + 0.1 * w)).astype(BF), m, v


def kernel(tile, x, dy, wg, wu, wd, *refs):
    moments, (ng, nu, nd), new_moments, (a_s, at_s, do_s, dot_s, h_s, da_s, act_s, dg_s, du_s, wgb, wub, wdb, gg, gu, gd,
           pg, pd, d2s_g, d2s_d, d2r_g, d2r_d, sr_g, sr_d, sl_g, sl_d, rl_g, rl_d, rr_g, rr_d, nw_g, nw_d,
           og, ou, od, wsem, lsem, d2_ss, d2_rs, sr_ss, rl_rs, sl_ss, rr_rs, own_s, ar_ss, al_ss, ap_ss, al_rs, ar_rs, ap_rs,
           mg, mu, md, vg, vu, vd, msem) = refs[:6], refs[6:9], refs[9:15], refs[15:]
    held = (mg, mu, md, vg, vu, vd)
    dev = lax.axis_index("dp")
    z, k = dev // 2, dev % 2
    right, left, other = {"dp": (dev + 2) % 8}, {"dp": (dev + 6) % 8}, {"dp": z * 2 + 1 - k}
    tiles = h_s.shape[0] // tile

    barrier = pltpu.get_barrier_semaphore()
    for to in (right, left, other):
        pl.semaphore_signal(barrier, inc=1, device_id=to, device_id_type=pl.DeviceIdType.MESH)
    pl.semaphore_wait(barrier, 3)

    def remote(src, dst, ss, rs, to):
        return pltpu.make_async_remote_copy(src_ref=src, dst_ref=dst, send_sem=ss, recv_sem=rs, device_id=to,
                                            device_id_type=pl.DeviceIdType.MESH)

    def ok(j):
        return (j >= 0) & (j < CHUNKS)

    def weights(j):
        layer, _, c1, c2 = where(j)
        slot = j % 2
        out = []
        for i, c in enumerate((c1, c2)):
            here = slice(128 * i, 128 * i + 128)
            out.append((wg.at[layer, :, pl.ds(c, 128)], wgb.at[slot, :, here]))
            out.append((wu.at[layer, :, pl.ds(c, 128)], wub.at[slot, :, here]))
            out.append((wd.at[layer, pl.ds(c, 128), :], wdb.at[slot, here, :]))
        return [pltpu.make_async_copy(src, dst, wsem.at[slot, i]) for i, (src, dst) in enumerate(out)]

    def over_tiles(body):
        @pl.loop(0, tiles)
        def _(i):
            body(pl.ds(pl.multiple_of(i * tile, tile), tile))

    def unit(h):
        return lax.rsqrt(jnp.mean(h * h, -1, keepdims=True) + 1e-6)

    here = pltpu.make_async_copy(x, h_s, lsem.at[0])
    mine = pl.ds(pl.multiple_of(80 * dev, 16), 80)
    later = [pltpu.make_async_copy(wg.at[:, mine, :], og, lsem.at[2]), pltpu.make_async_copy(wu.at[:, mine, :], ou, lsem.at[3]),
             pltpu.make_async_copy(wd.at[:, pl.ds(pl.multiple_of(256 * dev, 256), 256), :], od, lsem.at[4]),
             pltpu.make_async_copy(dy, do_s, lsem.at[1])]
    later += [pltpu.make_async_copy(src, dst, msem.at[i]) for i, (src, dst) in enumerate(zip(moments, held, strict=True))]
    for c in [here] + weights(8) + later:
        c.start()
    here.wait()

    def enter(rows):
        h = h_s[rows, :].astype(F32)
        a_s[0, rows, :] = (h * unit(h)).astype(BF)
        da_s[rows, :] = jnp.zeros((tile, D), F32)

    over_tiles(enter)

    @pl.loop(8, 16)
    def _(j):
        slot = j % 2
        for c in weights(j):
            c.wait()
        for c in weights((j + 1) % 16):
            c.start()

        def forward(rows):
            a = a_s[0, rows, :]
            gate, up = dot(a, wgb[slot]), dot(a, wub[slot])
            da_s[rows, :] += dot((gate * jax.nn.sigmoid(gate) * up).astype(BF), wdb[slot])

        over_tiles(forward)

    def leave(rows):
        h = (h_s[rows, :].astype(F32) + da_s[rows, :].astype(BF).astype(F32)).astype(BF)
        h_s[rows, :] = h
        h = h.astype(F32)
        a_s[1, rows, :] = (h * unit(h)).astype(BF)
        at_s[1, :, rows] = a_s[1, rows, :].T
        dot_s[:, rows] = do_s[rows, :].T
        da_s[rows, :] = jnp.zeros((tile, D), F32)

    for c in later:
        c.wait()
    over_tiles(leave)

    def chunk(t):
        slot, layer = t % 2, 1 - t // 8

        @pl.when(t == 8)
        def _():
            def back(rows):
                h = h_s[rows, :].astype(F32)
                da = da_s[rows, :].astype(BF).astype(F32)
                r = unit(h)
                dh = r * da - h * (r * r * r * jnp.mean(h * da, -1, keepdims=True))
                do_s[rows, :] = (do_s[rows, :].astype(F32) + dh.astype(BF).astype(F32)).astype(BF)
                dot_s[:, rows] = do_s[rows, :].T

            over_tiles(back)

        @pl.when(t == 4)
        def _():
            def turn(rows):
                at_s[0, :, rows] = a_s[0, rows, :].T

            over_tiles(turn)

        for c in weights(t):
            c.wait()

        @pl.when(t + 1 < CHUNKS)
        def _():
            for c in weights(t + 1):
                c.start()

        def through(rows):
            a, d = a_s[layer, rows, :], do_s[rows, :]
            gate, up = dot(a, wgb[slot]), dot(a, wub[slot])
            dact = dot_t(d, wdb[slot]).astype(BF).astype(F32)
            sig = jax.nn.sigmoid(gate)
            silu = gate * sig
            act_s[rows, :] = (silu * up).astype(BF)
            du_s[rows, :] = (dact * silu).astype(BF)
            dg_s[rows, :] = (dact * up * (sig * (1 + gate * (1 - sig)))).astype(BF)

        over_tiles(through)

        @pl.when(t < 8)
        def _():
            def into(rows):
                da_s[rows, :] += dot_t(dg_s[rows, :], wgb[slot]) + dot_t(du_s[rows, :], wub[slot])

            over_tiles(into)

    def gradients(t):
        slot, keep, layer = t % 2, t % HELD, 1 - t // 8
        gg[...] = dot(at_s[layer], dg_s[...])
        gu[...] = dot(at_s[layer], du_s[...])
        gd[...] = dot(dot_s[...], act_s[...])
        for b in range(4):
            mine = pl.ds(pl.multiple_of(160 * b + 80 * k, 16), 80)
            its = pl.ds(pl.multiple_of(160 * b + 80 * (1 - k), 16), 80)
            for i, g in enumerate((gg, gu)):
                pg[keep, b, 80 * i : 80 * i + 80, :] = g[mine, :]
                d2s_g[slot, b, 80 * i : 80 * i + 80, :] = g[its, :].astype(BF)
        pd[keep] = gd[:, pl.ds(pl.multiple_of(128 * k, 128), 128)].T
        d2s_d[slot] = gd[:, pl.ds(pl.multiple_of(128 * (1 - k), 128), 128)].T.astype(BF)
        for c in swap(t):
            c.start()

    def swap(j):
        slot, keep = j % 2, j % SLOTS
        return [remote(d2s_g.at[slot], d2r_g.at[keep], d2_ss.at[slot, 0], d2_rs.at[keep, 0], other),
                remote(d2s_d.at[slot], d2r_d.at[keep], d2_ss.at[slot, 1], d2_rs.at[keep, 1], other)]

    def to_right(j, b):
        return remote(sr_g.at[j % 2, b - 1], rl_g.at[j % SLOTS, b - 1], sr_ss.at[j % 2, b - 1], rl_rs.at[j % SLOTS, b - 1], right)

    def to_right_d(j):
        return remote(sr_d.at[j % 2], rl_d.at[j % SLOTS], sr_ss.at[j % 2, 3], rl_rs.at[j % SLOTS, 3], right)

    def to_left(j, b):
        return remote(sl_g.at[j % 2, b], rr_g.at[j % SLOTS, b], sl_ss.at[j % 2, b], rr_rs.at[j % SLOTS, b], left)

    def to_left_d(j):
        return remote(sl_d.at[j % 2], rr_d.at[j % SLOTS], sl_ss.at[j % 2, 3], rr_rs.at[j % SLOTS, 3], left)

    def reduce(t):
        j = t - 1

        @pl.when(ok(j))
        def _():
            for c in swap(j):
                c.wait()
            keep, came = j % HELD, j % SLOTS
            for b in range(4):
                pg[keep, b] += d2r_g[came, b].astype(F32)
            pd[keep] += d2r_d[came].astype(F32)

        jr, jl = t - 1 - z, t - 4 + z
        sr, sl = chip_of(jr, k), chip_of(jl, k)

        def rightward(b):
            @pl.when(ok(jr) & (z > 0) & (z <= b))
            def _():
                to_right(jr, b).wait_recv()
                pg[jr % HELD, b] += rl_g[jr % SLOTS, b - 1].astype(F32)

            @pl.when(ok(jr) & (z < b))
            def _():
                sr_g[jr % 2, b - 1] = pg[jr % HELD, b].astype(BF)
                to_right(jr, b).start()

            @pl.when(ok(jr - 1) & (z < b))
            def _():
                to_right(jr - 1, b).wait_send()

        def leftward(b):
            @pl.when(ok(jl) & (z < 3) & (z >= b))
            def _():
                to_left(jl, b).wait_recv()
                pg[jl % HELD, b] += rr_g[jl % SLOTS, b].astype(F32)

            @pl.when(ok(jl) & (z > b))
            def _():
                sl_g[jl % 2, b] = pg[jl % HELD, b].astype(BF)
                to_left(jl, b).start()

            @pl.when(ok(jl - 1) & (z > b))
            def _():
                to_left(jl - 1, b).wait_send()

        for b in (3, 2, 1):
            rightward(b)
            leftward(3 - b)

        @pl.when(ok(jr) & (z > 0) & (z <= sr))
        def _():
            to_right_d(jr).wait_recv()
            pd[jr % HELD] += rl_d[jr % SLOTS].astype(F32)

        @pl.when(ok(jr) & (z < sr))
        def _():
            sr_d[jr % 2] = pd[jr % HELD].astype(BF)
            to_right_d(jr).start()

        @pl.when(ok(jr - 1) & (z < chip_of(jr - 1, k)))
        def _():
            to_right_d(jr - 1).wait_send()

        @pl.when(ok(jl) & (z < 3) & (z >= sl))
        def _():
            to_left_d(jl).wait_recv()
            pd[jl % HELD] += rr_d[jl % SLOTS].astype(F32)

        @pl.when(ok(jl) & (z > sl))
        def _():
            sl_d[jl % 2] = pd[jl % HELD].astype(BF)
            to_left_d(jl).start()

        @pl.when(ok(jl - 1) & (z > chip_of(jl - 1, k)))
        def _():
            to_left_d(jl - 1).wait_send()

    def update(j):
        layer, h, c1, c2 = where(j)
        keep, slot = j % HELD, j % 2
        for i, (w, m, v) in enumerate(((og, mg, vg), (ou, mu, vu))):
            for n, c in enumerate((c1, c2)):
                at = (layer, slice(None), pl.ds(c, 128))
                g = pg[keep, z, 80 * i : 80 * i + 80, 128 * n : 128 * n + 128].astype(BF).astype(F32)
                new, m[at], v[at] = adam(w[at].astype(F32), m[at], v[at], g)
                nw_g[slot, 80 * i : 80 * i + 80, 128 * n : 128 * n + 128] = new

        @pl.when(chip_of(j, k) == z)
        def _():
            at = (layer, pl.ds(pl.multiple_of(h * 128, 128), 128), slice(None))
            g = pd[keep].astype(BF).astype(F32)
            new, md[at], vd[at] = adam(od[at].astype(F32), md[at], vd[at], g)
            nw_d[slot] = new

    def windows(j, origin, core):
        layer, h, c1, c2 = where(j)
        rows = pl.ds(pl.multiple_of(160 * origin + 80 * core, 16), 80)
        down = pl.ds(pl.multiple_of((2 * origin + core) * 256 + 128 * h, 128), 128)
        return [n.at[layer, rows, pl.ds(c, 128)] for n in (ng, nu) for c in (c1, c2)], nd.at[layer, down, :], chip_of(j, core) == origin

    def sources(j, a, origin):
        if a == 0:
            slot = j % 2
            return [nw_g.at[slot, 80 * i : 80 * i + 80, 128 * n : 128 * n + 128] for i in range(2) for n in range(2)], nw_d.at[slot]
        return windows(j, origin, k)[:2]

    def start(j, a, origin, ss, rs, to):
        into, into_d, has = windows(j, origin, k)
        src, src_d = sources(j, a, origin)
        for x, y in zip(src, into, strict=True):
            remote(x, y, ss.at[j % 2, a, 0], rs.at[j % SLOTS, a, 0], to).start()

        @pl.when(has)
        def _():
            remote(src_d, into_d, ss.at[j % 2, a, 1], rs.at[j % SLOTS, a, 1], to).start()

    def finish(has, gate_up, down):
        pltpu.make_async_copy(nw_g.at[0], nw_g.at[0], gate_up).wait()

        @pl.when(has)
        def _():
            pltpu.make_async_copy(nw_d.at[0], nw_d.at[0], down).wait()

    def gather(t):
        def each(j, a, origin, side, what):
            valid = ok(j) & (origin >= 0) & (origin < 4)
            has = chip_of(j, k) == origin

            @pl.when(valid)
            def _():
                if side in (0, 1) and a < 3:
                    pl.when(z < 3)(lambda: what(j, a, origin, has, ar_ss, al_rs, right))
                if side in (0, 2) and a < 3:
                    pl.when(z > 0)(lambda: what(j, a, origin, has, al_ss, ar_rs, left))
                what(j, a, origin, has, ap_ss.at[side], ap_rs.at[side], other)

        def waited(j, a, origin, has, ss, rs, to):
            finish(has, ss.at[j % 2, a, 0], ss.at[j % 2, a, 1])

        def begun(j, a, origin, has, ss, rs, to):
            start(j, a, origin, ss, rs, to)

        j = t - 4

        @pl.when(ok(j - 1))
        def _():
            finish(chip_of(j - 1, k) == z, own_s.at[(j - 1) % 2, 0], own_s.at[(j - 1) % 2, 1])

        each(j - 1, 0, z, 0, waited)

        @pl.when(ok(j))
        def _():
            update(j)
            into, into_d, has = windows(j, z, k)
            src, src_d = sources(j, 0, z)
            for x, y in zip(src, into, strict=True):
                pltpu.make_async_copy(x, y, own_s.at[j % 2, 0]).start()

            @pl.when(has)
            def _():
                pltpu.make_async_copy(src_d, into_d, own_s.at[j % 2, 1]).start()

        each(j, 0, z, 0, begun)

        for a in (1, 2, 3):
            ja = t - 4 - a
            for side, origin, rs in ((1, z - a, al_rs), (2, z + a, ar_rs)):
                each(ja - 1, a, origin, side, waited)

                @pl.when(ok(ja) & (origin >= 0) & (origin < 4))
                def _():
                    finish(chip_of(ja, k) == origin, rs.at[ja % SLOTS, a - 1, 0], rs.at[ja % SLOTS, a - 1, 1])

                each(ja, a, origin, side, begun)

        for a in (0, 1, 2, 3):
            jp = t - 5 - a
            for side, origin in ((0, z),) if a == 0 else ((1, z - a), (2, z + a)):
                @pl.when(ok(jp) & (origin >= 0) & (origin < 4))
                def _():
                    finish(chip_of(jp, 1 - k) == origin, ap_rs.at[side, jp % SLOTS, a, 0], ap_rs.at[side, jp % SLOTS, a, 1])

    back_out = [pltpu.make_async_copy(src, dst, msem.at[i]) for i, (src, dst) in enumerate(zip(held, new_moments, strict=True))]

    @pl.loop(0, CHUNKS + 8)
    def _(t):
        pl.when(t < CHUNKS)(lambda: chunk(t))
        reduce(t)
        pl.when(t < CHUNKS)(lambda: gradients(t))
        gather(t)

        @pl.when(t == CHUNKS + 3)
        def _():
            for c in back_out:
                c.start()

    for c in back_out:
        c.wait()


def step_kernel(tokens):
    tile = min(tokens, 1024)
    sds = jax.ShapeDtypeStruct
    hbm = pl.BlockSpec(memory_space=pltpu.HBM)
    wide, tall, block, down = (2, D, FF), (2, FF, D), (2, D // 8, FF), (2, FF // 8, D)
    gu, dn = (160, 256), (128, D)
    V, dma = pltpu.VMEM, pltpu.SemaphoreType.DMA
    scratch = [
        V((2, tokens, D), BF), V((2, D, tokens), BF), V((tokens, D), BF), V((D, tokens), BF), V((tokens, D), BF), V((tokens, D), F32),
        V((tokens, 256), BF), V((tokens, 256), BF), V((tokens, 256), BF),
        V((2, D, 256), BF), V((2, D, 256), BF), V((2, 256, D), BF), V((D, 256), F32), V((D, 256), F32), V((D, 256), F32),
        V((HELD, 4, *gu), F32), V((HELD, *dn), F32), V((2, 4, *gu), BF), V((2, *dn), BF), V((SLOTS, 4, *gu), BF), V((SLOTS, *dn), BF),
        V((2, 3, *gu), BF), V((2, *dn), BF), V((2, 3, *gu), BF), V((2, *dn), BF),
        V((SLOTS, 3, *gu), BF), V((SLOTS, *dn), BF), V((SLOTS, 3, *gu), BF), V((SLOTS, *dn), BF),
        V((2, *gu), BF), V((2, *dn), BF), V(block, BF), V(block, BF), V(down, BF),
        dma((2, 6)), dma((5,)), dma((2, 2)), dma((SLOTS, 2)), dma((2, 4)), dma((SLOTS, 4)), dma((2, 4)), dma((SLOTS, 4)),
        dma((2, 2)), dma((2, 3, 2)), dma((2, 3, 2)), dma((3, 2, 4, 2)), dma((SLOTS, 3, 2)), dma((SLOTS, 3, 2)), dma((3, SLOTS, 4, 2)),
        *[V(s, F32) for s in (block, block, down)] * 2, dma((6,)),
    ]
    return pl.pallas_call(
        functools.partial(kernel, tile),
        out_shape=[sds(wide, BF), sds(wide, BF), sds(tall, BF)] + [sds(s, F32) for s in (block, block, down)] * 2,
        in_specs=[hbm] * 11,
        out_specs=[hbm] * 9,
        scratch_shapes=scratch,
        compiler_params=pltpu.CompilerParams(collective_id=0, has_side_effects=True, vmem_limit_bytes=64 * 2**20),
        name="step",
    )


def solution(mesh):
    def step(x, dy, wg, wu, wd, *moments):
        return tuple(step_kernel(x.shape[1])(x[0], dy[0], wg, wu, wd, *moments))

    mine, whole, rows = P(("rep", "dp"), None, None), P(None, None, None), P(None, "dp", None)
    return jax.shard_map(
        step, mesh=mesh, in_specs=(mine, mine) + (whole,) * 3 + (rows,) * 6,
        out_specs=(P("rep", None, None),) * 3 + (P("rep", "dp", None),) * 6, check_vma=False,
    )
```

time: 321 us -> 285 us (0.89)
  matrix products: 33.5 us -> 0 us
  other arithmetic: 7.61 us -> 0.01 us
  Pallas kernels: 257 us -> 263 us
    dot_general x2 -> x0, matrix products: 33.5 us -> none  [dot(): lax.dot_general(a, b, (((1,), (0,)), ((), ())), preferred_element_type=F32)]
    pallas_call x1, Pallas kernels: 257 us -> 263 us  [step(): return tuple(step_kernel(x.shape[1])(x[0], dy[0], wg, wu, wd, *moments))]
    convert_element_type x1 -> x0, other arithmetic: 5.12 us -> none  [normed(): return (wide * scale).astype(BF)]
    dynamic_slice x2 -> x0, local copies, waits for them, and re-layouts: 4.48 us -> none  [step(): lax.dynamic_slice_in_dim(w, me * (w.shape[1] // 8), w.shape[1] // 8, 1)]
    unnamed x31 -> x27, local copies, waits for them, and re-layouts: 17.6 us -> 20.9 us
where the time goes in v2:
time: 285 us
  Pallas kernels  263 us (92%)
  local copies, waits for them, and re-layouts  20.9 us (7%)
    pallas_call x1, Pallas kernels, step(): return tuple(step_kernel(x.shape[1])(x[0], dy[0], wg, wu, wd, *moments))  263 us
    unnamed x27, local copies, waits for them, and re-layouts  20.9 us

profile of v2, /device:TPU:0, one launch (start us, length us, event | category | flops | bytes accessed | tf_op | source)
XLA Modules:
  0.0 284.7 jit_solution(15943207891626718246)
XLA Ops:
  0.6 263.2 %step.1 = (bf16[2,640,2048]{2,1,0:T(8,128)(2,1)}, bf16[2,640,2048]{2,1,0:T(8,128)(2,1)}, bf16[2,2048,640]{2,1,0:T(8,128)(2,1)}, f32[2,80,2048]{2,1,0:T(8,128)}, ...) custom-call(bf16[2048,640]{1,0:T(8,128)(2,1)} %bitcast.4, ...), custom_call_target="tpu_custom_call" | custom-call | tf_op jit(solution)/shard_map/step/pallas_call | solution.py:443
  263.8 0.0 copy-start
  263.8 0.0 slice-start
  263.8 6.2 %copy.29 = bf16[2,640,2048]{2,1,0:T(8,128)(2,1)} copy(bf16[2,640,2048]{2,1,0:T(8,128)(2,1)} %get-tuple-element.18) | data formatting | bytes 10485760
  270.0 0.0 copy-done
  270.0 0.0 slice-start.1
  270.0 2.4 copy.30
  272.4 0.0 slice-done
  272.4 0.0 slice-done.1
  272.4 0.0 copy-start.6
  272.4 2.4 copy.31
  274.7 0.0 copy-done.6
  274.7 0.0 copy-start.5
  274.7 1.1 copy.32
  275.8 0.7 copy-done.5
  276.5 0.0 copy-start.4
  276.5 1.1 copy.33
  277.6 0.7 copy-done.4
  278.3 0.0 copy-start.3
  278.3 1.1 copy.34
  279.4 0.7 copy-done.3
  280.1 0.0 copy-start.2
  280.1 1.1 copy.35
  281.2 0.7 copy-done.2
  281.9 0.0 copy-start.1
  281.9 1.1 copy.36
  283.0 0.7 copy-done.1
  283.7 1.1 copy.37
  (1 shorter events, 0.0 us)
Async XLA Ops:
  263.8 6.2 %copy-start = (bf16[2,640,2048]{2,1,0:T(8,128)(2,1)S(1)}, bf16[2,640,2048]{2,1,0:T(8,128)(2,1)}, u32[]{:S(2)}) copy-start(bf16[2,640,2048]{2,1,0:T(8,128)(2,1)} %get-tuple-element.19) | copy-start | bytes 15728644
  263.8 8.5 %slice-start = ((s8[5242880]{0:T(1024)(128)(4,1)}), s8[4194304]{0:T(1024)(128)(4,1)S(1)}, s32[]{:S(2)}) async-start(s8[5242880]{0:T(1024)(128)(4,1)} %bitcast.2), calls=%async_computation | async-start | bytes 8388608
  270.0 2.4 slice-start.1
  272.4 2.4 copy-start.6
  274.7 1.8 copy-start.5
  276.5 1.8 copy-start.4
  278.3 1.8 copy-start.3
  280.1 1.8 copy-start.2
  281.9 1.8 copy-start.1

commit v3 on v2

--- a/solution.py
+++ b/solution.py
@@ -167,6 +167,9 @@
             dg_s[rows, :] = (dact * up * (sig * (1 + gate * (1 - sig)))).astype(BF)
 
         over_tiles(through)
+
+    def inward(t):
+        slot = t % 2
 
         @pl.when(t < 8)
         def _():
@@ -396,6 +399,7 @@
     def _(t):
         pl.when(t < CHUNKS)(lambda: chunk(t))
         reduce(t)
+        pl.when(t < 8)(lambda: inward(t))
         pl.when(t < CHUNKS)(lambda: gradients(t))
         gather(t)
 

time: 285 us -> 284 us (level)
  no operation moved by 1% of the time
where the time goes in v3:
time: 284 us; the launch traced here: 283 us
  Pallas kernels  262 us (92%)
  local copies, waits for them, and re-layouts  20.9 us (7%)
    pallas_call x1, Pallas kernels, step(): return tuple(step_kernel(x.shape[1])(x[0], dy[0], wg, wu, wd, *moments))  262 us
    unnamed x27, local copies, waits for them, and re-layouts  20.9 us

profile of v3, /device:TPU:0, one launch (start us, length us, event | category | flops | bytes accessed | tf_op | source)
XLA Modules:
  0.0 283.2 jit_solution(10070204517795464698)
XLA Ops:
  0.6 261.6 %step.1 = (bf16[2,640,2048]{2,1,0:T(8,128)(2,1)}, bf16[2,640,2048]{2,1,0:T(8,128)(2,1)}, bf16[2,2048,640]{2,1,0:T(8,128)(2,1)}, f32[2,80,2048]{2,1,0:T(8,128)}, ...) custom-call(bf16[2048,640]{1,0:T(8,128)(2,1)} %bitcast.4, ...), custom_call_target="tpu_custom_call" | custom-call | tf_op jit(solution)/shard_map/step/pallas_call | solution.py:447
  262.3 0.0 copy-start
  262.3 0.0 slice-start
  262.3 6.2 %copy.29 = bf16[2,640,2048]{2,1,0:T(8,128)(2,1)} copy(bf16[2,640,2048]{2,1,0:T(8,128)(2,1)} %get-tuple-element.18) | data formatting | bytes 10485760
  268.5 0.0 copy-done
  268.5 0.0 slice-start.1
  268.5 2.4 copy.30
  270.8 0.0 slice-done
  270.8 0.0 slice-done.1
  270.8 0.0 copy-start.6
  270.8 2.4 copy.31
  273.2 0.0 copy-done.6
  273.2 0.0 copy-start.5
  273.2 1.1 copy.32
  274.3 0.7 copy-done.5
  275.0 0.0 copy-start.4
  275.0 1.1 copy.33
  276.0 0.7 copy-done.4
  276.8 0.0 copy-start.3
  276.8 1.1 copy.34
  277.8 0.7 copy-done.3
  278.6 0.0 copy-start.2
  278.6 1.1 copy.35
  279.6 0.7 copy-done.2
  280.4 0.0 copy-start.1
  280.4 1.1 copy.36
  281.4 0.7 copy-done.1
  282.1 1.1 copy.37
  (1 shorter events, 0.0 us)
Async XLA Ops:
  262.3 6.2 %copy-start = (bf16[2,640,2048]{2,1,0:T(8,128)(2,1)S(1)}, bf16[2,640,2048]{2,1,0:T(8,128)(2,1)}, u32[]{:S(2)}) copy-start(bf16[2,640,2048]{2,1,0:T(8,128)(2,1)} %get-tuple-element.19) | copy-start | bytes 15728644
  262.3 8.5 %slice-start = ((s8[5242880]{0:T(1024)(128)(4,1)}), s8[4194304]{0:T(1024)(128)(4,1)S(1)}, s32[]{:S(2)}) async-start(s8[5242880]{0:T(1024)(128)(4,1)} %bitcast.2), calls=%async_computation | async-start | bytes 8388608
  268.5 2.4 slice-start.1
  270.8 2.4 copy-start.6
  273.2 1.8 copy-start.5
  275.0 1.8 copy-start.4
  276.8 1.8 copy-start.3
  278.6 1.8 copy-start.2
  280.4 1.8 copy-start.1
